TPU v7x, 32 devices: a whole 2x2x4 slice. The times are simulated.
32 devices in a mesh: ep: 8 (over z, y), tp: 4 (over x, core).
Axes of the slice: x: 2, y: 2, z: 4, core: 2. Of those that a mesh axis runs over, the one named last changes fastest.
Arguments:
- tokens: bfloat16 [4096, 2048], P(('ep', 'tp')), may hold values from -6 to 6
- norm_gain: float32 [2048], replicated, may hold values from 0.1 to 1.9
- expert_ids: int32 [4096, 6], P(('ep', 'tp')), may hold values from 0 to 15, as said below
- slot_index: int32 [4096, 6], P(('ep', 'tp')), may hold values from 0 to 63, as said below
- dropped: int32 [4096, 6], P(('ep', 'tp')), may hold values from 0 to 1, as said below
- gates: float32 [4096, 6], P(('ep', 'tp')), may hold values from 0.05 to 0.8
- w_gate: bfloat16 [16, 2048, 704], P('ep', None, 'tp'), may hold values from -0.125 to 0.125
- w_up: bfloat16 [16, 2048, 704], P('ep', None, 'tp'), may hold values from -0.125 to 0.125
- w_down: bfloat16 [16, 2048, 704], P('ep', None, 'tp'), may hold values from -0.21875 to 0.21875
- shared_gate: bfloat16 [2048, 1408], P(None, 'tp'), may hold values from -0.125 to 0.125
- shared_up: bfloat16 [2048, 1408], P(None, 'tp'), may hold values from -0.125 to 0.125
- shared_down: bfloat16 [1408, 2048], replicated, may hold values from -0.15625 to 0.15625
Outputs:
- layer_out: bfloat16 [4096, 2048], P(('ep', 'tp'))
Inputs may be any that keep to these rules, and one draw needn't show every extreme that they name: `expert_ids`: each token names 6 different experts; some expert has 64 kept pairs from the tokens of every device. `slot_index`: for a kept pair, its place among the slots of its expert for the tokens of its device (the tokens n with one value of n // 128); the kept pairs of one device and one expert have distinct places; 0 for a dropped pair. `dropped`: 1 for the pairs of a device and an expert beyond the 64 that are kept.
All inputs are finite; a program needn't handle non-finite values.
Results may differ from a plain program's by a relative error of at most 0.0054.
Values may be sent and summed in bfloat16 or wider, within the bound.
A program may use at most 128 MiB of HBM per device.

v0:
```python
import jax
import jax.numpy as jnp
from jax import lax
from jax.sharding import PartitionSpec as P

TOP = 6
EXP_DEV = 2
TOK_DEV = 128


norm_eps = 1e-06


def swiglu(left, right):
    return jax.nn.silu(left) * right


def on_device(
    tokens,
    norm_gain,
    expert_ids,
    slot_index,
    dropped,
    gates,
    w_gate,
    w_up,
    w_down,
    shared_gate,
    shared_up,
    shared_down,
):
    n_expert_groups = lax.axis_size("ep")
    experts = EXP_DEV * n_expert_groups
    capacity = TOK_DEV * TOP * 4 // (experts * 3)
    model_width = tokens.shape[1]
    local_rows = tokens.shape[0]
    values = tokens.astype(jnp.float32)
    scale = lax.rsqrt(jnp.mean(values * values, axis=-1, keepdims=True) + norm_eps)
    normed = (values * scale * norm_gain).astype(jnp.bfloat16)
    destination_position = expert_ids * capacity + slot_index
    kept_pair = dropped == 0
    matrix_breadth = lax.iota(jnp.int32, experts * capacity)
    matches = (destination_position[:, :, None] == matrix_breadth[None, None, :]) & kept_pair[
        :, :, None
    ]
    dispatch_table = jnp.any(matches, axis=1).astype(jnp.bfloat16)
    outgoing = lax.dot_general(
        dispatch_table, normed, (((0,), (0,)), ((), ())), preferred_element_type=jnp.float32
    ).astype(jnp.bfloat16)
    boxes = outgoing.reshape(n_expert_groups, EXP_DEV, capacity, model_width)
    received = lax.all_to_all(boxes, "ep", split_axis=0, concat_axis=0, tiled=True)
    gate_all = lax.all_gather(w_gate, "tp", axis=2, tiled=True)
    up_all = lax.all_gather(w_up, "tp", axis=2, tiled=True)
    down_all = lax.all_gather(w_down, "tp", axis=2, tiled=True)
    gate_act = jnp.einsum("iecd,edf->iecf", received, gate_all, preferred_element_type=jnp.float32)
    up_act = jnp.einsum("iecd,edf->iecf", received, up_all, preferred_element_type=jnp.float32)
    hidden = swiglu(gate_act, up_act).astype(jnp.bfloat16)
    expert_out = jnp.einsum(
        "iecf,edf->iecd", hidden, down_all, preferred_element_type=jnp.float32
    ).astype(jnp.bfloat16)
    returned_output = lax.all_to_all(expert_out, "ep", split_axis=0, concat_axis=0, tiled=True)
    returned_rows = returned_output.reshape(experts * capacity, model_width)
    shard_piece = lax.all_gather(normed, "tp", axis=0, tiled=True)
    gate_act = jnp.dot(shard_piece, shared_gate, preferred_element_type=jnp.float32)
    up_act = jnp.dot(shard_piece, shared_up, preferred_element_type=jnp.float32)
    partial_hidden = swiglu(gate_act, up_act).astype(jnp.bfloat16)
    whole_hidden = lax.all_to_all(partial_hidden, "tp", split_axis=0, concat_axis=1, tiled=True)
    shared_out = jnp.dot(whole_hidden, shared_down, preferred_element_type=jnp.float32)
    safe_target = jnp.where(kept_pair, destination_position, 0)
    picked = jnp.take(returned_rows, safe_target.reshape(-1), axis=0).reshape(
        local_rows, TOP, model_width
    )
    kept_weights = jnp.where(kept_pair, gates, jnp.float32(0.0))
    routed = jnp.sum(picked.astype(jnp.float32) * kept_weights[:, :, None], axis=1)
    return (values + shared_out + routed).astype(jnp.bfloat16)


def solution(mesh):
    placed = (
        P(("ep", "tp"), None),
        P(),
        P(("ep", "tp"), None),
        P(("ep", "tp"), None),
        P(("ep", "tp"), None),
        P(("ep", "tp"), None),
        P("ep", None, "tp"),
        P("ep", None, "tp"),
        P("ep", None, "tp"),
        P(None, "tp"),
        P(None, "tp"),
        P(),
    )
    return jax.shard_map(
        on_device, mesh=mesh, in_specs=placed, out_specs=P(("ep", "tp"), None), check_vma=False
    )
```

profile of v0, /device:TPU:0, one launch (start us, length us, event | category | flops | bytes accessed | tf_op | source)
XLA Modules:
  0.0 298.9 jit_solution(15551164740821854965)
XLA Ops:
  6.5 0.0 copy-start
  6.5 0.0 copy-start.1
  6.5 0.0 copy-start.3
  6.5 0.0 copy-start.6
  6.5 0.0 copy-start.7
  6.6 0.0 all-gather.9.cloned.1.call-start
  6.6 0.7 all-gather.9.cloned.1.call-update
  7.3 0.0 all-gather.11.cloned.1.call-start
  7.3 0.7 all-gather.11.cloned.1.call-update
  8.0 0.0 all-gather.7.cloned.1.call-start
  8.1 0.7 all-gather.7.cloned.1.call-update
  8.8 0.0 copy-done.1
  8.8 0.2 fusion.29
  9.0 0.0 copy-done.3
  9.0 0.2 fusion.31
  9.2 0.0 copy-start.2
  9.2 0.0 copy-done.6
  9.2 0.0 copy-done.5
  9.2 0.0 copy-done.7
  9.3 0.6 fusion.15
  9.9 1.3 convolution_convert_fusion
  11.2 100.4 %all_to_all.29 = bf16[8,2,64,2048]{3,2,1,0:T(8,128)(2,1)} all-to-all(bf16[8,2,64,2048]{3,2,1,0:T(8,128)(2,1)S(1)} %bitcast.62), channel_id=1, replica_groups=mesh['ep'=8,'tp'=4] {'ep'}, dimensions={0} | all-to-all | bytes 8388608 | tf_op jit(solution)/shard_map/all_to_all | solution.py:51
  111.5 0.0 copy-done.2
  111.5 9.2 %fusion.2 = f32[2,8,64,704]{3,2,1,0:T(8,128)} fusion(bf16[2,2048,704]{1,2,0:T(8,128)(2,1)} %all-gather.9.cloned.1.call-done, bf16[8,2,64,2048]{3,2,1,0:T(8,128)(2,1)} %all_to_all.29), kind=kOutput, calls=%fused_computation.4 | convolution fusion | flops 2952790016 | bytes 12845056 | tf_op jit(solution)/shard_map/iecd,edf->iecf/dot_general | solution.py:56
  120.7 24.3 %all-gather.7.cloned.1.call-done = bf16[2,2048,704]{1,2,0:T(8,128)(2,1)} async-done(((bf16[2,2048,176]{1,2,0:T(8,128)(2,1)}), bf16[2,2048,704]{1,2,0:T(8,128)(2,1)}) %all-gather.7.cloned.1.call-update) | async-done | bytes 5767184 | tf_op jit(solution)/shard_map/all_gather | solution.py:52
  145.0 13.1 %convert_bitcast_fusion = bf16[8,2,64,2048]{3,2,0,1:T(8,128)(2,1)} fusion(bf16[2,2048,704]{1,2,0:T(8,128)(2,1)} %all-gather.11.cloned.1.call-done, f32[2,8,64,704]{3,2,1,0:T(8,128)} %fusion.2, bf16[2,2048,704]{1,2,0:T(8,128)(2,1)} %all-gather.7.cloned.1.call-done, bf16[8,2,64,2048]{3,2,1,0:T(8,128)(2,1)} %all_to_all.29), kind=kOutput, calls=%fused_computation.8 | convolution fusion | flops 5912002560 | bytes 22806528 | tf_op jit(solution)/shard_map/iecf,edf->iecd/dot_general | solution.py:58
  158.1 4.7 %copy.39 = bf16[8,2,64,2048]{3,2,1,0:T(8,128)(2,1)} copy(bf16[8,2,64,2048]{3,2,0,1:T(8,128)(2,1)} %convert_bitcast_fusion) | data formatting | bytes 8388608 | tf_op jit(solution)/shard_map/convert_element_type | solution.py:60
  162.9 5.6 %all-to-all-start.2 = ((bf16[8,2,64,2048]{3,2,1,0:T(8,128)(2,1)}), bf16[8,2,64,2048]{3,2,1,0:T(8,128)(2,1)}, u32[]{:S(2)}, u32[]{:S(2)}) async-start(bf16[8,2,64,2048]{3,2,1,0:T(8,128)(2,1)} %copy.39), calls=%async_computation.2 | async-start | bytes 8388608 | tf_op jit(solution)/shard_map/all_to_all | solution.py:61
  168.5 0.0 all-gather.5.cloned.1.call-start
  168.6 0.5 all-gather.5.cloned.1.call-update
  169.1 0.1 copy.40
  169.2 0.1 reshape.66
  169.4 0.0 copy-done.4
  169.4 0.1 copy.41
  169.5 0.1 copy.36
  169.7 24.0 %all-gather.5.cloned.1.call-done = bf16[512,2048]{1,0:T(8,128)(2,1)} async-done(((bf16[128,2048]{1,0:T(8,128)(2,1)}), bf16[512,2048]{1,0:T(8,128)(2,1)}) %all-gather.5.cloned.1.call-update) | async-done | bytes 2097168 | tf_op jit(solution)/shard_map/all_gather | solution.py:63
  193.7 0.0 copy-done
  193.7 2.7 fusion.34
  196.4 0.0 copy-done.8
  196.4 2.4 fusion.28
  198.8 0.8 copy.55
  199.6 62.6 %all-to-all-done.2 = bf16[8,2,64,2048]{3,2,1,0:T(8,128)(2,1)} async-done(((bf16[8,2,64,2048]{3,2,1,0:T(8,128)(2,1)}), bf16[8,2,64,2048]{3,2,1,0:T(8,128)(2,1)}, u32[]{:S(2)}, u32[]{:S(2)}) %all-to-all-start.2) | async-done | bytes 4194336 | tf_op jit(solution)/shard_map/all_to_all | solution.py:61
  262.2 3.6 %all-to-all-start = ((bf16[4,128,352]{1,2,0:T(8,128)(2,1)}), bf16[4,128,352]{1,2,0:T(8,128)(2,1)S(1)}, u32[]{:S(2)}, u32[]{:S(2)}) async-start(bf16[4,128,352]{1,2,0:T(8,128)(2,1)} %bitcast.61), calls=%async_computation | async-start | bytes 720896 | tf_op jit(solution)/shard_map/all_to_all | solution.py:67
  265.9 9.9 %gather_fusion = bf16[768,2048]{1,0:T(8,128)(2,1)} fusion(bf16[1024,2048]{1,0:T(8,128)(2,1)} %bitcast.12, s32[1024]{0:T(1024)S(1)} %pad_clamp_fusion), kind=kCustom, calls=%fused_computation | custom fusion | bytes 6294528 | tf_op jit(solution)/shard_map/jit(_take)/gather | solution.py:70
  275.7 6.2 %gather.7 = bf16[128,6,2048]{2,1,0:T(8,128)(2,1)} reshape(bf16[768,2048]{1,0:T(8,128)(2,1)} %gather_fusion) | data formatting | bytes 6291456 | tf_op jit(solution)/shard_map/jit(_take)/gather | solution.py:70
  282.0 6.0 %multiply_reduce_fusion = f32[128,2048]{1,0:T(8,128)S(1)} fusion(f32[128,6]{1,0:T(8,128)S(1)} %copy.41, bf16[128,6,2048]{2,1,0:T(8,128)(2,1)} %gather.7, pred[128,6]{1,0:T(8,128)(4,1)S(1)} %copy.36), kind=kLoop, calls=%fused_computation.1 | loop fusion | flops 6029312 | bytes 4198144 | tf_op jit(solution)/shard_map/reduce_sum | solution.py:74
  287.9 0.0 all-to-all-done
  287.9 4.4 %fusion.17 = bf16[128,2048]{1,0:T(8,128)(2,1)} fusion(f32[128,2048]{1,0:T(8,128)S(1)} %multiply_reduce_fusion, bf16[128,1408]{0,1:T(8,128)(2,1)S(1)} %bitcast.63, bf16[1408,2048]{1,0:T(8,128)(2,1)} %param.23, bf16[128,2048]{1,0:T(8,128)(2,1)S(1)} %copy-done.1), kind=kOutput, calls=%fused_computation.24 | convolution fusion | flops 739246080 | bytes 8224768 | tf_op jit(solution)/shard_map/dot_general | solution.py:68
  (10 shorter events, 0.1 us)
Async XLA Ops:
  6.5 187.1 %copy-start = (bf16[2048,352]{0,1:T(8,128)(2,1)S(1)}, bf16[2048,352]{0,1:T(8,128)(2,1)}, u32[]{:S(2)}) copy-start(bf16[2048,352]{0,1:T(8,128)(2,1)} %param.21) | copy-start | bytes 4325380
  6.5 2.2 copy-start.1
  6.5 2.4 copy-start.3
  6.5 2.7 copy-start.6
  6.5 2.7 copy-start.5
  6.5 2.7 copy-start.7
  6.6 105.0 %all-gather.9.cloned.1.call-start = ((), (), s32[]{:S(2)}) async-start(), calls=%async_computation.5 | async-start | bytes 7208960 | tf_op jit(solution)/shard_map/all_gather | solution.py:53
  7.3 113.4 %all-gather.11.cloned.1.call-start = ((), (), s32[]{:S(2)}) async-start(), calls=%async_computation.6 | async-start | bytes 7208960 | tf_op jit(solution)/shard_map/all_gather | solution.py:54
  8.0 137.0 %all-gather.7.cloned.1.call-start = ((), (), s32[]{:S(2)}) async-start(), calls=%async_computation.4 | async-start | bytes 7208960 | tf_op jit(solution)/shard_map/all_gather | solution.py:52
  9.2 102.4 %copy-start.2 = (bf16[128,2048]{1,0:T(8,128)(2,1)}, bf16[128,2048]{1,0:T(8,128)(2,1)S(1)}, u32[]{:S(2)}) copy-start(bf16[128,2048]{1,0:T(8,128)(2,1)S(1)} %fusion.31) | copy-start | bytes 1572868
  162.9 6.5 %copy-start.4 = (f32[128,6]{0,1:T(8,128)S(1)}, f32[128,6]{0,1:T(8,128)}, u32[]{:S(2)}) copy-start(f32[128,6]{0,1:T(8,128)} %param.17) | copy-start | bytes 9220
  162.9 99.3 %all-to-all-start.2 = ((bf16[8,2,64,2048]{3,2,1,0:T(8,128)(2,1)}), bf16[8,2,64,2048]{3,2,1,0:T(8,128)(2,1)}, u32[]{:S(2)}, u32[]{:S(2)}) async-start(bf16[8,2,64,2048]{3,2,1,0:T(8,128)(2,1)} %copy.39), calls=%async_computation.2 | async-start | bytes 8388608 | tf_op jit(solution)/shard_map/all_to_all | solution.py:61
  168.5 25.1 %all-gather.5.cloned.1.call-start = ((), (), s32[]{:S(2)}) async-start(), calls=%async_computation.3 | async-start | bytes 2621440 | tf_op jit(solution)/shard_map/all_gather | solution.py:63
  193.7 2.7 copy-start.8
  262.2 25.7 %all-to-all-start = ((bf16[4,128,352]{1,2,0:T(8,128)(2,1)}), bf16[4,128,352]{1,2,0:T(8,128)(2,1)S(1)}, u32[]{:S(2)}, u32[]{:S(2)}) async-start(bf16[4,128,352]{1,2,0:T(8,128)(2,1)} %bitcast.61), calls=%async_computation | async-start | bytes 720896 | tf_op jit(solution)/shard_map/all_to_all | solution.py:67
Sparse Core Ops, SparseCore 0:
  8.9 46.0 all-gather.8
  56.6 43.3 all-gather.10
  101.6 43.3 all-gather.6
  170.6 23.0 all-gather.4
where the time goes:
time: 300 us; the launch traced here: 299 us
  waiting for transfers between devices  114 us (38%)
  blocking collectives  100 us (33%)
  matrix products  33.2 us (11%)
  local copies, waits for them, and re-layouts  22.2 us (7%)
  between operations  13.3 us (4%)
  starting transfers between devices  9.44 us (3%)
  other arithmetic  6.97 us (2%)
    all_to_all x1, blocking collectives, on_device(): lax.all_to_all(boxes, 'ep', split_axis=0, concat_axis=0, tiled=True)  100 us
    all_to_all x1, waiting for transfers between devices, on_device(): lax.all_to_all(expert_out, 'ep', split_axis=0, concat_axis=0, tiled=True)  62.6 us
    all_gather x1, waiting for transfers between devices, on_device(): gate_all = lax.all_gather(w_gate, 'tp', axis=2, tiled=True)  24.3 us
    all_gather x1, waiting for transfers between devices, on_device(): shard_piece = lax.all_gather(normed, 'tp', axis=0, tiled=True)  24 us
    gather x2, local copies, waits for them, and re-layouts, on_device(): jnp.take(returned_rows, safe_target.reshape(-1), axis=0)  16.1 us
    dot_general x1, matrix products, on_device(): jnp.einsum('iecf,edf->iecd', hidden, down_all, preferred_element_type=jnp...  13.1 us
    dot_general x1, matrix products, on_device(): jnp.einsum('iecd,edf->iecf', received, up_all, preferred_element_type=jnp...  9.17 us
  transfers between devices with their start and end apart: 6, of which 3 were waited for; matrix products, arithmetic and copies ran while one was open for 13% of the time, Pallas kernels for 0%

commit v1 on v0

--- a/solution.py
+++ b/solution.py
@@ -1,7 +1,393 @@
+import functools
+
 import jax
 import jax.numpy as jnp
 from jax import lax
+from jax.experimental import pallas as pl
+from jax.experimental.pallas import tpu as pltpu
 from jax.sharding import PartitionSpec as P
+
+MESH = pl.DeviceIdType.MESH
+CORES = 2
+COLS = 2
+VMEM_BYTES = 62 * 1024 * 1024
+PIECES = 4
+
+NT = (((1,), (1,)), ((), ()))
+NN = (((1,), (0,)), ((), ()))
+
+
+def dot(a, b, dims):
+    return lax.dot_general(a, b, dims, preferred_element_type=jnp.float32)
+
+
+def flip(index, mask, size):
+    out, bit = 0, 1
+    while bit < size:
+        digit = (index // bit) % 2
+        out = out + (1 - digit if mask & bit else digit) * bit
+        bit *= 2
+    return out
+
+
+def layer_kernel(
+    n_rows_z,
+    tokens,
+    gain,
+    ids,
+    dropped,
+    gates,
+    w_gate,
+    w_up,
+    w_down,
+    s_gate,
+    s_up,
+    s_down,
+    out,
+    xb,
+    wtb,
+    gu,
+    db,
+    hb,
+    sb,
+    sg,
+    su,
+    sd,
+    sh,
+    whid,
+    ysend,
+    yrecv,
+    ypart,
+    zsend,
+    zrecv,
+    w_send,
+    w_recv,
+    own_sem,
+    z_send,
+    z_recv,
+    y_send,
+    y_recv,
+    t_send,
+    t_recv,
+    h_send,
+    h_recv,
+    ry_send,
+    ry_recv,
+    rz_send,
+    rz_recv,
+):
+    ep, tp = lax.axis_index("ep"), lax.axis_index("tp")
+    z, y = ep // COLS, ep % COLS
+    x, core = tp // CORES, tp % CORES
+    rows, width = tokens.shape
+    experts = w_gate.shape[0]
+    hid = w_gate.shape[1]
+    shid = s_gate.shape[0]
+    piece = width // PIECES
+    mate = (ep, x * CORES + 1 - core)
+    across = (ep, (1 - x) * CORES + core)
+    diagonal = (ep, (1 - x) * CORES + 1 - core)
+    beside = (z * COLS + 1 - y, tp)
+    along = [None] + [(flip(z, r, n_rows_z) * COLS + y, tp) for r in range(1, n_rows_z)]
+
+    barrier = pltpu.get_barrier_semaphore()
+    peers = [mate, across, diagonal, beside] + along[1:]
+    for peer in peers:
+        pl.semaphore_signal(barrier, inc=1, device_id=peer, device_id_type=MESH)
+
+    def local(src, dst, sem):
+        c = pltpu.make_async_copy(src, dst, sem)
+        c.start()
+        return c
+
+    own = []
+    chunks = []
+    for e in range(experts):
+        for m, source in enumerate((w_gate, w_up)):
+            chunks.append((source.at[e], functools.partial(lambda e, m, s: gu.at[e, m, s], e, m)))
+    first_down = len(chunks)
+    for c in range(PIECES):
+        cut = pl.ds(c * piece, piece)
+        chunks.append(
+            (w_down.at[:, :, cut], functools.partial(lambda cut, s: db.at[:, s, :, cut], cut))
+        )
+    for k, (source, place) in enumerate(chunks):
+        own.append(local(source, place(0), own_sem.at[k]))
+    n = len(chunks)
+    shared_in = [local(s_gate, sg, own_sem.at[n]), local(s_up, su, own_sem.at[n + 1])]
+    who = [tp, mate[1], across[1], diagonal[1]]
+    shared_down_in = [
+        local(
+            s_down.at[pl.ds(pl.multiple_of(who[s] * shid, 16), shid), :],
+            sd.at[s],
+            own_sem.at[n + 2 + s],
+        )
+        for s in range(4)
+    ]
+
+    pl.semaphore_wait(barrier, len(peers))
+    sent = []
+
+    def remote(src, dst, ssem, rsem, peer):
+        c = pltpu.make_async_remote_copy(
+            src_ref=src,
+            dst_ref=dst,
+            send_sem=ssem,
+            recv_sem=rsem,
+            device_id=peer,
+            device_id_type=MESH,
+        )
+        c.start()
+        sent.append(c)
+        return c
+
+    far = [remote(s, p(2), w_send.at[1, k], w_recv.at[1, k], across) for k, (s, p) in enumerate(chunks)]
+    near = [remote(s, p(1), w_send.at[0, k], w_recv.at[0, k], mate) for k, (s, p) in enumerate(chunks)]
+
+    values = tokens[...].astype(jnp.float32)
+    scale = lax.rsqrt(jnp.mean(values * values, axis=-1, keepdims=True) + 1e-06)
+    xb[0, 0] = (values * scale * gain[...]).astype(jnp.bfloat16)
+    table = jnp.zeros(wtb.shape[2:], jnp.float32)
+    rows_of = lax.broadcasted_iota(jnp.int32, wtb.shape[2:], 0)
+    for k in range(ids.shape[0]):
+        hit = (ids[k : k + 1, :] == rows_of) & (dropped[k : k + 1, :] == 0)
+        table = table + jnp.where(hit, gates[k : k + 1, :], 0.0)
+    wtb[0, 0] = table
+
+    rz, ry = [None], []
+    for r in range(1, n_rows_z):
+        rz.append(
+            (
+                remote(xb.at[0, 0], xb.at[0, r], z_send.at[0, r], z_recv.at[0, r], along[r]),
+                remote(wtb.at[0, 0], wtb.at[0, r], z_send.at[1, r], z_recv.at[1, r], along[r]),
+            )
+        )
+
+    def to_side(r):
+        if r:
+            for c in rz[r]:
+                c.wait_recv()
+        ry.append(
+            (
+                remote(xb.at[0, r], xb.at[1, r], y_send.at[0, r], y_recv.at[0, r], beside),
+                remote(wtb.at[0, r], wtb.at[1, r], y_send.at[1, r], y_recv.at[1, r], beside),
+            )
+        )
+
+    to_side(0)
+    share_near = remote(xb.at[0, 0], sb.at[1], t_send.at[0], t_recv.at[0], mate)
+    share_far = remote(xb.at[0, 0], sb.at[2], t_send.at[1], t_recv.at[1], across)
+
+    passed = []
+
+    def pass_on(k):
+        far[k].wait_recv()
+        place = chunks[k][1]
+        passed.append(remote(place(2), place(3), w_send.at[2, k], w_recv.at[2, k], mate))
+
+    def column(side, r, e):
+        line = jnp.sum(
+            jnp.where(rows_of == ep * experts + e, wtb[side, r], 0.0), axis=0, keepdims=True
+        )
+        return jnp.transpose(jnp.broadcast_to(line, (rows, rows)))[:, 0:1]
+
+    def hidden(first, count, pair, e_first, e_count):
+        def body(i, carry):
+            e = e_first + i % e_count
+            r = first + i // e_count
+            left = jnp.concatenate([xb[0, r], xb[1, r]], axis=0)
+            g = dot(left, gu[e, 0, 2 * pair : 2 * pair + 2].reshape(2 * hid, width), NT)
+            u = dot(left, gu[e, 1, 2 * pair : 2 * pair + 2].reshape(2 * hid, width), NT)
+            weight = jnp.concatenate([column(0, r, e), column(1, r, e)], axis=0)
+            h = (g * jax.nn.sigmoid(g) * u * weight).astype(jnp.bfloat16)
+            hb[0, e, pair, r] = h[:rows]
+            hb[1, e, pair, r] = h[rows:]
+            return carry
+
+        lax.fori_loop(0, count * e_count, body, 0)
+
+    def shared_hidden(pair):
+        left = xb[0, 0] if pair == 0 else sb[2]
+        left = jnp.concatenate([left, sb[2 * pair + 1]], axis=0)
+        g = dot(left, sg[...], NT)
+        u = dot(left, su[...], NT)
+        h = (g * jax.nn.sigmoid(g) * u).astype(jnp.bfloat16)
+        sh[2 * pair] = h[:rows]
+        sh[2 * pair + 1] = h[rows:]
+
+    for k in range(first_down):
+        own[k].wait()
+        near[k].wait_recv()
+    to_side(1)
+    for c in ry[0]:
+        c.wait_recv()
+    hidden(0, 1, 0, 0, experts)
+    for c in shared_in:
+        c.wait()
+    share_near.wait_recv()
+    shared_hidden(0)
+    shs = [remote(sh.at[1], whid.at[1], h_send.at[0], h_recv.at[0], mate)]
+    pass_on(0)
+    for c in ry[1]:
+        c.wait_recv()
+    hidden(1, 1, 0, 0, experts)
+    to_side(2)
+    pass_on(1)
+    passed[0].wait_recv()
+    passed[1].wait_recv()
+    hidden(0, 2, 1, 0, 1)
+    for c in ry[2]:
+        c.wait_recv()
+    hidden(2, 1, 0, 0, experts)
+    hidden(2, 1, 1, 0, 1)
+    to_side(3)
+    pass_on(2)
+    for c in ry[3]:
+        c.wait_recv()
+    hidden(3, 1, 0, 0, experts)
+    hidden(3, 1, 1, 0, 1)
+    pass_on(3)
+    passed[2].wait_recv()
+    passed[3].wait_recv()
+    hidden(0, n_rows_z, 1, 1, 1)
+
+    ryd, rzd = [], []
+
+    def down(c, side):
+        cut = pl.ds(c * piece, piece)
+
+        def body(q, carry):
+            total = None
+            for e in range(experts):
+                for pair in range(2):
+                    left = hb[side, e, pair, pl.ds(2 * q, 2)].reshape(2 * rows, 2 * hid)
+                    right = db[e, 2 * pair : 2 * pair + 2, :, cut].reshape(2 * hid, piece)
+                    part = dot(left, right, NN)
+                    total = part if total is None else total + part
+            total = total.reshape(2, rows, piece)
+            if side:
+                ysend[c, pl.ds(2 * q, 2)] = total.astype(jnp.bfloat16)
+            else:
+                ypart[c, pl.ds(2 * q, 2)] = total
+            return carry
+
+        lax.fori_loop(0, n_rows_z // 2, body, 0)
+
+    def turn(c):
+        ryd[c].wait_recv()
+        for r in range(1, n_rows_z):
+            both = ypart[c, r] + yrecv[c, r].astype(jnp.float32)
+            zsend[c, r] = both.astype(jnp.bfloat16)
+        rzd.append(
+            [
+                remote(zsend.at[c, r], zrecv.at[c, r], rz_send.at[c, r], rz_recv.at[c, r], along[r])
+                for r in range(1, n_rows_z)
+            ]
+        )
+
+    for c in range(PIECES):
+        k = first_down + c
+        own[k].wait()
+        near[k].wait_recv()
+        pass_on(k)
+        passed[k].wait_recv()
+        down(c, 1)
+        ryd.append(remote(ysend.at[c], yrecv.at[c], ry_send.at[c], ry_recv.at[c], beside))
+        down(c, 0)
+        if c:
+            turn(c - 1)
+
+    share_far.wait_recv()
+    share_on = remote(sb.at[2], sb.at[3], t_send.at[2], t_recv.at[2], mate)
+    share_on.wait_recv()
+    shared_hidden(1)
+    shs.append(remote(sh.at[2], whid.at[2], h_send.at[1], h_recv.at[1], across))
+    shs.append(remote(sh.at[3], whid.at[3], h_send.at[2], h_recv.at[2], diagonal))
+    turn(PIECES - 1)
+    for c in shared_down_in:
+        c.wait()
+    for c in shs:
+        c.wait_recv()
+    for c in range(PIECES):
+        cut = pl.ds(c * piece, piece)
+        total = tokens[:, cut].astype(jnp.float32) + dot(sh[0], sd[0, :, cut], NN)
+        for s in range(1, 4):
+            total = total + dot(whid[s], sd[s, :, cut], NN)
+        total = total + (ypart[c, 0] + yrecv[c, 0].astype(jnp.float32))
+        for r in range(1, n_rows_z):
+            rzd[c][r - 1].wait_recv()
+            total = total + zrecv[c, r].astype(jnp.float32)
+        out[:, cut] = total.astype(out.dtype)
+    for c in sent:
+        c.wait_send()
+
+
+def scratch_of(n_rows_z, rows, width, n_experts, experts, hid, shid):
+    bf, f4 = jnp.bfloat16, jnp.float32
+    piece = width // PIECES
+    lines = n_experts
+    pad = lambda v: -(-v // 128) * 128
+    shapes = [
+        ((COLS, n_rows_z, rows, width), bf),
+        ((COLS, n_rows_z, lines, rows), f4),
+        ((experts, 2, 4, hid, width), bf),
+        ((experts, 4, hid, width), bf),
+        ((COLS, experts, 2, n_rows_z, rows, 2 * hid), bf),
+        ((4, rows, width), bf),
+        ((shid, width), bf),
+        ((shid, width), bf),
+        ((4, shid, width), bf),
+        ((4, rows, shid), bf),
+        ((4, rows, shid), bf),
+        ((PIECES, n_rows_z, rows, piece), bf),
+        ((PIECES, n_rows_z, rows, piece), bf),
+        ((PIECES, n_rows_z, rows, piece), f4),
+        ((PIECES, n_rows_z, rows, piece), bf),
+        ((PIECES, n_rows_z, rows, piece), bf),
+    ]
+    total = 0
+    for dims, kind in shapes:
+        size = pad(dims[-1]) * jnp.dtype(kind).itemsize
+        for d in dims[:-1]:
+            size *= d
+        total += size
+    n = 2 * experts + PIECES
+    dma = pltpu.SemaphoreType.DMA
+    sems = [dma((3, n)), dma((3, n)), dma((n + 6,))]
+    sems += [dma((2, n_rows_z)) for _ in range(4)]
+    sems += [dma((3,)) for _ in range(4)]
+    sems += [dma((PIECES,)) for _ in range(2)]
+    sems += [dma((PIECES, n_rows_z)) for _ in range(2)]
+    return [pltpu.VMEM(d, k) for d, k in shapes] + sems, total
+
+
+def fused(n_rows_z, scratch, tokens, gain, ids, slot, dropped, gates, wg, wu, wd, sg, su, sd):
+    vmem = pl.BlockSpec(memory_space=pltpu.VMEM)
+    hbm = pl.BlockSpec(memory_space=pl.ANY)
+    return pl.pallas_call(
+        functools.partial(layer_kernel, n_rows_z),
+        out_shape=jax.ShapeDtypeStruct(tokens.shape, tokens.dtype),
+        in_specs=[vmem] * 5 + [hbm] * 6,
+        out_specs=vmem,
+        scratch_shapes=scratch,
+        compiler_params=pltpu.CompilerParams(
+            collective_id=0, has_side_effects=True, vmem_limit_bytes=VMEM_BYTES
+        ),
+        name="moe_layer",
+    )(
+        tokens,
+        gain[None, :],
+        ids.T,
+        dropped.T,
+        gates.T,
+        wg.transpose(0, 2, 1),
+        wu.transpose(0, 2, 1),
+        wd.transpose(0, 2, 1),
+        sg.T,
+        su.T,
+        sd,
+    )
+
 
 TOP = 6
 EXP_DEV = 2
@@ -76,6 +462,7 @@
 
 
 def solution(mesh):
+    ep, tp = mesh.shape["ep"], mesh.shape["tp"]
     placed = (
         P(("ep", "tp"), None),
         P(),
@@ -90,6 +477,24 @@
         P(None, "tp"),
         P(),
     )
+
+    def layer(*args):
+        tokens, w_gate, shared_gate = args[0], args[6], args[9]
+        n_rows_z = ep // COLS
+        scratch, size = scratch_of(
+            n_rows_z,
+            tokens.shape[0],
+            tokens.shape[1],
+            ep * w_gate.shape[0],
+            w_gate.shape[0],
+            w_gate.shape[2],
+            shared_gate.shape[1],
+        )
+        spare = 8 * 1024 * 1024
+        if tp == 2 * CORES and n_rows_z == 4 and size + spare < VMEM_BYTES:
+            return fused(n_rows_z, scratch, *args)
+        return on_device(*args)
+
     return jax.shard_map(
-        on_device, mesh=mesh, in_specs=placed, out_specs=P(("ep", "tp"), None), check_vma=False
+        layer, mesh=mesh, in_specs=placed, out_specs=P(("ep", "tp"), None), check_vma=False
     )

time: 300 us -> 146 us (0.49)
  Pallas kernels: 0 us -> 144 us
  waiting for transfers between devices: 114 us -> 0 us
  blocking collectives: 100 us -> 0 us
  matrix products: 33.2 us -> 0 us
  local copies, waits for them, and re-layouts: 22.2 us -> 1.88 us
  between operations: 13.3 us -> 0.01 us
  starting transfers between devices: 9.44 us -> 0 us
  other arithmetic: 6.97 us -> 0 us
    pallas_call x0 -> x1, Pallas kernels: none -> 144 us  [fused(): pl.pallas_call(functools.partial(layer_kernel, n_rows_z), out_shape=jax.S...]
    all_to_all x1 -> x0, blocking collectives: 100 us -> none  [on_device(): lax.all_to_all(boxes, 'ep', split_axis=0, concat_axis=0, tiled=True)]
    all_to_all x2 -> x0, waiting for transfers between devices: 62.6 us -> none  [the longest x1 62.6 us: on_device(): lax.all_to_all(expert_out, 'ep', split_axis=0, concat_axis=0, tiled=True)]
    all_gather x4 -> x0, waiting for transfers between devices: 48.3 us -> none  [the longest x1 24.3 us: on_device(): gate_all = lax.all_gather(w_gate, 'tp', axis=2, tiled=True)]
    dot_general x6 -> x0, matrix products: 33.2 us -> none  [the longest x1 13.1 us: on_device(): jnp.einsum('iecf,edf->iecd', hidden, down_all, preferred_element_type=jnp...]
    gather x2 -> x0, local copies, waits for them, and re-layouts: 16.1 us -> none  [on_device(): jnp.take(returned_rows, safe_target.reshape(-1), axis=0)]
    all_to_all x2 -> x0, starting transfers between devices: 9.29 us -> none  [the longest x1 5.65 us: on_device(): lax.all_to_all(expert_out, 'ep', split_axis=0, concat_axis=0, tiled=True)]
    reduce_sum x2 -> x0, other arithmetic: 6.14 us -> none  [the longest x1 5.95 us: on_device(): jnp.sum(picked.astype(jnp.float32) * kept_weights[:, :, None], axis=1)]
  transfers between devices with their start and end apart: 6 -> 0, of which waited for: 3 -> 0; matrix products, arithmetic and copies ran while one was open for 13% -> 0% of each run, Pallas kernels for 0% -> 0%
where the time goes in v1:
time: 146 us
  Pallas kernels  144 us (99%)
  local copies, waits for them, and re-layouts  1.88 us (1%)
    pallas_call x1, Pallas kernels, fused(): pl.pallas_call(functools.partial(layer_kernel, n_rows_z), out_shape=jax.S...  144 us

profile of v1, /device:TPU:0, one launch (start us, length us, event | category | flops | bytes accessed | tf_op | source)
XLA Modules:
  0.0 146.1 jit_solution(5490473171478467042)
XLA Ops:
  0.0 144.2 %moe_layer.1 = bf16[128,2048]{1,0:T(8,128)(2,1)} custom-call(bf16[128,2048]{1,0:T(8,128)(2,1)} %tokens.1, f32[1,2048]{1,0:T(1,128)} %bitcast.14, s32[6,128]{1,0:T(8,128)} %bitcast.15, s32[6,128]{1,0:T(8,128)} %bitcast.16, f32[6,128]{1,0:T(8,128)} %bitcast.17, bf16[2,176,2048]{2,1,0:T(8,128)(2,1)} %bitcast.9, bf16[2,176,2048]{2,1,0:T(8,128)(2,1)} %bitcast.10, ...), custom_call_target="tpu_custom_call" | custom-call | tf_op jit(solution)/shard_map/moe_layer/pallas_call | solution.py:367
  144.2 1.9 %copy.13 = bf16[128,2048]{1,0:T(8,128)(2,1)} copy(bf16[128,2048]{1,0:T(8,128)(2,1)} %moe_layer.1) | data formatting | bytes 1048576

commit v2 on v1

--- a/solution.py
+++ b/solution.py
@@ -11,7 +11,7 @@
 CORES = 2
 COLS = 2
 VMEM_BYTES = 62 * 1024 * 1024
-PIECES = 4
+PIECES = 8
 
 NT = (((1,), (1,)), ((), ()))
 NN = (((1,), (0,)), ((), ()))
@@ -47,6 +47,7 @@
     xb,
     wtb,
     gu,
+    ga,
     db,
     hb,
     sb,
@@ -141,7 +142,15 @@
         sent.append(c)
         return c
 
-    far = [remote(s, p(2), w_send.at[1, k], w_recv.at[1, k], across) for k, (s, p) in enumerate(chunks)]
+    early = first_down + PIECES // 2
+
+    def send_far(first, last):
+        for k in range(first, last):
+            source, place = chunks[k]
+            far.append(remote(source, place(2), w_send.at[1, k], w_recv.at[1, k], across))
+
+    far = []
+    send_far(0, early)
     near = [remote(s, p(1), w_send.at[0, k], w_recv.at[0, k], mate) for k, (s, p) in enumerate(chunks)]
 
     values = tokens[...].astype(jnp.float32)
@@ -154,29 +163,39 @@
         table = table + jnp.where(hit, gates[k : k + 1, :], 0.0)
     wtb[0, 0] = table
 
+    half = rows // 2
+    parts = [(wtb, ())] + [(xb, (pl.ds(i * half, half),)) for i in range(2)]
+
+    def part_of(i, side, r):
+        ref, cut = parts[i]
+        return ref.at[(side, r) + cut]
+
     rz, ry = [None], []
     for r in range(1, n_rows_z):
         rz.append(
-            (
-                remote(xb.at[0, 0], xb.at[0, r], z_send.at[0, r], z_recv.at[0, r], along[r]),
-                remote(wtb.at[0, 0], wtb.at[0, r], z_send.at[1, r], z_recv.at[1, r], along[r]),
+            [
+                remote(
+                    part_of(i, 0, 0), part_of(i, 0, r), z_send.at[i, r], z_recv.at[i, r], along[r]
+                )
+                for i in range(3)
+            ]
+        )
+
+    def to_side(r):
+        ry.append([])
+        for i in range(3):
+            if r:
+                rz[r][i].wait_recv()
+            ry[r].append(
+                remote(
+                    part_of(i, 0, r), part_of(i, 1, r), y_send.at[i, r], y_recv.at[i, r], beside
+                )
             )
-        )
-
-    def to_side(r):
-        if r:
-            for c in rz[r]:
-                c.wait_recv()
-        ry.append(
-            (
-                remote(xb.at[0, r], xb.at[1, r], y_send.at[0, r], y_recv.at[0, r], beside),
-                remote(wtb.at[0, r], wtb.at[1, r], y_send.at[1, r], y_recv.at[1, r], beside),
-            )
-        )
 
     to_side(0)
     share_near = remote(xb.at[0, 0], sb.at[1], t_send.at[0], t_recv.at[0], mate)
     share_far = remote(xb.at[0, 0], sb.at[2], t_send.at[1], t_recv.at[1], across)
+    send_far(early, n)
 
     passed = []
 
@@ -191,12 +210,23 @@
         )
         return jnp.transpose(jnp.broadcast_to(line, (rows, rows)))[:, 0:1]
 
-    def hidden(first, count, pair, e_first, e_count):
+    def gate_only(first, count, e):
+        def body(r, carry):
+            left = jnp.concatenate([xb[0, r], xb[1, r]], axis=0)
+            ga[r] = dot(left, gu[e, 0, 2:4].reshape(2 * hid, width), NT)
+            return carry
+
+        lax.fori_loop(first, first + count, body, 0)
+
+    def hidden(first, count, pair, e_first, e_count, stored=False):
         def body(i, carry):
             e = e_first + i % e_count
             r = first + i // e_count
             left = jnp.concatenate([xb[0, r], xb[1, r]], axis=0)
-            g = dot(left, gu[e, 0, 2 * pair : 2 * pair + 2].reshape(2 * hid, width), NT)
+            if stored:
+                g = ga[r]
+            else:
+                g = dot(left, gu[e, 0, 2 * pair : 2 * pair + 2].reshape(2 * hid, width), NT)
             u = dot(left, gu[e, 1, 2 * pair : 2 * pair + 2].reshape(2 * hid, width), NT)
             weight = jnp.concatenate([column(0, r, e), column(1, r, e)], axis=0)
             h = (g * jax.nn.sigmoid(g) * u * weight).astype(jnp.bfloat16)
@@ -242,14 +272,16 @@
     hidden(2, 1, 1, 0, 1)
     to_side(3)
     pass_on(2)
+    passed[2].wait_recv()
+    gate_only(0, 3, 1)
     for c in ry[3]:
         c.wait_recv()
     hidden(3, 1, 0, 0, experts)
     hidden(3, 1, 1, 0, 1)
+    gate_only(3, 1, 1)
     pass_on(3)
-    passed[2].wait_recv()
     passed[3].wait_recv()
-    hidden(0, n_rows_z, 1, 1, 1)
+    hidden(0, n_rows_z, 1, 1, 1, stored=True)
 
     ryd, rzd = [], []
 
@@ -296,24 +328,32 @@
         down(c, 0)
         if c:
             turn(c - 1)
-
-    share_far.wait_recv()
-    share_on = remote(sb.at[2], sb.at[3], t_send.at[2], t_recv.at[2], mate)
-    share_on.wait_recv()
-    shared_hidden(1)
-    shs.append(remote(sh.at[2], whid.at[2], h_send.at[1], h_recv.at[1], across))
-    shs.append(remote(sh.at[3], whid.at[3], h_send.at[2], h_recv.at[2], diagonal))
-    turn(PIECES - 1)
+        if c == PIECES - 3:
+            share_far.wait_recv()
+            share_on = remote(sb.at[2], sb.at[3], t_send.at[2], t_recv.at[2], mate)
+            share_on.wait_recv()
+            shared_hidden(1)
+            shs.append(remote(sh.at[2], whid.at[2], h_send.at[1], h_recv.at[1], across))
+            shs.append(remote(sh.at[3], whid.at[3], h_send.at[2], h_recv.at[2], diagonal))
+
     for c in shared_down_in:
         c.wait()
     for c in shs:
         c.wait_recv()
-    for c in range(PIECES):
-        cut = pl.ds(c * piece, piece)
+
+    def base(c, carry):
+        cut = pl.ds(pl.multiple_of(c * piece, piece), piece)
         total = tokens[:, cut].astype(jnp.float32) + dot(sh[0], sd[0, :, cut], NN)
         for s in range(1, 4):
             total = total + dot(whid[s], sd[s, :, cut], NN)
-        total = total + (ypart[c, 0] + yrecv[c, 0].astype(jnp.float32))
+        ypart[c, 0] = ypart[c, 0] + total
+        return carry
+
+    lax.fori_loop(0, PIECES, base, 0)
+    turn(PIECES - 1)
+    for c in range(PIECES):
+        cut = pl.ds(c * piece, piece)
+        total = ypart[c, 0] + yrecv[c, 0].astype(jnp.float32)
         for r in range(1, n_rows_z):
             rzd[c][r - 1].wait_recv()
             total = total + zrecv[c, r].astype(jnp.float32)
@@ -331,6 +371,7 @@
         ((COLS, n_rows_z, rows, width), bf),
         ((COLS, n_rows_z, lines, rows), f4),
         ((experts, 2, 4, hid, width), bf),
+        ((n_rows_z, 2 * rows, 2 * hid), f4),
         ((experts, 4, hid, width), bf),
         ((COLS, experts, 2, n_rows_z, rows, 2 * hid), bf),
         ((4, rows, width), bf),
@@ -354,7 +395,7 @@
     n = 2 * experts + PIECES
     dma = pltpu.SemaphoreType.DMA
     sems = [dma((3, n)), dma((3, n)), dma((n + 6,))]
-    sems += [dma((2, n_rows_z)) for _ in range(4)]
+    sems += [dma((3, n_rows_z)) for _ in range(4)]
     sems += [dma((3,)) for _ in range(4)]
     sems += [dma((PIECES,)) for _ in range(2)]
     sems += [dma((PIECES, n_rows_z)) for _ in range(2)]
@@ -491,7 +532,7 @@
             shared_gate.shape[1],
         )
         spare = 8 * 1024 * 1024
-        if tp == 2 * CORES and n_rows_z == 4 and size + spare < VMEM_BYTES:
+        if tp == 2 * CORES and n_rows_z == 4 and w_gate.shape[0] == 2 and size + spare < VMEM_BYTES:
             return fused(n_rows_z, scratch, *args)
         return on_device(*args)
 

time: 146 us -> 141 us (0.966)
  Pallas kernels: 144 us -> 138 us
    pallas_call x1, Pallas kernels: 144 us -> 138 us  [fused(): pl.pallas_call(functools.partial(layer_kernel, n_rows_z), out_shape=jax.S...]
where the time goes in v2:
time: 141 us; the launch traced here: 140 us
  Pallas kernels  138 us (98%)
  local copies, waits for them, and re-layouts  1.88 us (1%)
    pallas_call x1, Pallas kernels, fused(): pl.pallas_call(functools.partial(layer_kernel, n_rows_z), out_shape=jax.S...  138 us

profile of v2, /device:TPU:0, one launch (start us, length us, event | category | flops | bytes accessed | tf_op | source)
XLA Modules:
  0.0 140.3 jit_solution(35618323193011592)
XLA Ops:
  0.0 138.4 %moe_layer.1 = bf16[128,2048]{1,0:T(8,128)(2,1)} custom-call(bf16[128,2048]{1,0:T(8,128)(2,1)} %tokens.1, f32[1,2048]{1,0:T(1,128)} %bitcast.14, s32[6,128]{1,0:T(8,128)} %bitcast.15, s32[6,128]{1,0:T(8,128)} %bitcast.16, f32[6,128]{1,0:T(8,128)} %bitcast.17, bf16[2,176,2048]{2,1,0:T(8,128)(2,1)} %bitcast.9, bf16[2,176,2048]{2,1,0:T(8,128)(2,1)} %bitcast.10, ...), custom_call_target="tpu_custom_call" | custom-call | tf_op jit(solution)/shard_map/moe_layer/pallas_call | solution.py:408
  138.5 1.9 %copy.13 = bf16[128,2048]{1,0:T(8,128)(2,1)} copy(bf16[128,2048]{1,0:T(8,128)(2,1)} %moe_layer.1) | data formatting | bytes 1048576
